TPU v7x, 32 devices: a whole 2x2x4 slice. The times are simulated.
32 devices in a mesh: pts: 8 (over z, y), hrs: 4 (over x, core).
Axes of the slice: x: 2, y: 2, z: 4, core: 2. Of those that a mesh axis runs over, the one named last changes fastest.
Arguments:
- fields: float32 [512, 65536], P(('pts', 'hrs')), may hold values from -2000 to 2000, as said below
- probes: float32 [256, 512], replicated, may hold values from -0.25 to 0.25
Outputs:
- basis_rows: float32 [256, 65536], P(None, ('pts', 'hrs'))
- coeffs: float32 [256, 512], replicated
Inputs may be any that keep to these rules, and one draw needn't show every extreme that they name: `fields`: every hour and every grid point carries its own scale, and the values are real-valued and never all zero.
All inputs are finite; a program needn't handle non-finite values.
Results may differ from a plain program's by a relative error of at most 0.00017.
Values sent between devices are 32-bit elements; how exact they have to be, the bound alone decides.
A program may use at most 64 MiB of HBM per device.

v0:
```python
import functools

import jax
import jax.numpy as jnp
from jax import lax
from jax.experimental import pallas as pl
from jax.experimental.pallas import tpu as pltpu
from jax.sharding import PartitionSpec as P

HI = lax.Precision.HIGHEST

def mm(a, b, dims):
    return lax.dot_general(a, b, (dims, ((), ())), precision=HI, preferred_element_type=jnp.float32)

def invert_block(block, group):
    b = block.shape[0]
    shape = (8, 2 * b)
    rows = lax.broadcasted_iota(jnp.int32, (b, 2 * b), 0)
    cols = lax.broadcasted_iota(jnp.int32, (b, 2 * b), 1)
    eye = (rows + b == cols).astype(jnp.float32)
    m = jnp.concatenate([block, eye[:, b:]], axis=1)
    strips = [m[8 * s:8 * s + 8] for s in range(b // 8)]
    srow = lax.broadcasted_iota(jnp.int32, shape, 0)
    for j in range(0, b, group):
        s0, r0 = divmod(j, 8)
        strip = strips[s0]
        pivots = [jnp.broadcast_to(strip[r0 + r:r0 + r + 1, :], shape) for r in range(group)]
        corner = [
            [jnp.broadcast_to(strip[r0 + r:r0 + r + 1, j + c:j + c + 1], shape) for c in range(r + 1)]
            for r in range(group)
        ]
        ratio = [[None] * group for _ in range(group)]
        scaled = []
        for r in range(group):
            inv = 1.0 / corner[r][r]
            for lo in range(r + 1, group):
                ratio[lo][r] = corner[lo][r] * inv
            for lo in range(r + 1, group):
                for c in range(r + 1, lo + 1):
                    corner[lo][c] = corner[lo][c] - ratio[lo][r] * corner[c][r]
                pivots[lo] = pivots[lo] - ratio[lo][r] * pivots[r]
            scaled.append(pivots[r] * inv)
        for s in range(s0, b // 8):
            if s == s0 and r0 + group == 8:
                new = strips[s]
            else:
                held = strips[s]
                f = []
                new = held
                for r in range(group):
                    fr = jnp.broadcast_to(held[:, j + r:j + r + 1], shape)
                    for c in range(r):
                        fr = fr - ratio[r][c] * f[c]
                    f.append(fr)
                    new = new - fr * scaled[r]
                if s == s0:
                    new = jnp.where(srow >= r0 + group, new, held)
            if s == s0:
                for r in range(group):
                    new = jnp.where(srow == r0 + r, pivots[r], new)
            strips[s] = new
    m = jnp.concatenate(strips, axis=0)
    d = jnp.sum(jnp.where(rows == cols, m, 0.0), axis=1, keepdims=True)
    return m[:, b:] * lax.rsqrt(d)


def factor_kernel(cross_ref, probes_ref, sk_ref, basis_ref, coeffs_ref, aug, winv):
    k = cross_ref.shape[0]
    b = 64
    aug[:, :k] = mm(cross_ref[...], probes_ref[...], ((1,), (1,)))
    rows = lax.broadcasted_iota(jnp.int32, (k, k), 0)
    cols = lax.broadcasted_iota(jnp.int32, (k, k), 1)
    aug[:, k:] = (rows == cols).astype(jnp.float32)
    for i in range(k // b):
        lo, hi = i * b, (i + 1) * b
        w = invert_block(aug[lo:hi, lo:hi], 8)
        done = mm(w, aug[lo:hi, :], ((1,), (0,)))
        winv[lo:hi, :] = done[:, k:]
        if hi < k:
            aug[hi:, :] = aug[hi:, :] - mm(done[:, hi:k], done, ((0,), (0,)))
    w = winv[...]
    coeffs_ref[...] = mm(w, cross_ref[...], ((1,), (0,)))
    n = sk_ref.shape[1]
    @pl.loop(0, n // 512)
    def _(t):
        c = pl.ds(pl.multiple_of(t * 512, 512), 512)
        basis_ref[:, c] = mm(w, sk_ref[:, c], ((1,), (0,)))

def finish(cross, probes, sk):
    k = cross.shape[0]
    v = pl.BlockSpec(memory_space=pltpu.VMEM)
    return pl.pallas_call(factor_kernel,
        out_shape=(jax.ShapeDtypeStruct(sk.shape, jnp.float32), jax.ShapeDtypeStruct(cross.shape, jnp.float32)),
        in_specs=[v, v, v], out_specs=(v, v),
        scratch_shapes=[pltpu.VMEM((k, 2 * k), jnp.float32), pltpu.VMEM((k, k), jnp.float32)],
        name="factor")(cross, probes, sk)


def sum_kernel(n_pts, n_hrs, lanes, cols, x_ref, out_ref, got1, part, got2, s1, r1, s2, r2, s3, r3, s4, r4):
    pts, hrs = lax.axis_index("pts"), lax.axis_index("hrs")
    rows, width = x_ref.shape
    q = rows // n_hrs
    parts = width // lanes
    per_row = lanes // cols

    def peer_hrs(o):
        return lax.rem(hrs + o, n_hrs)

    def peer_pts(o):
        return lax.rem(pts + o, n_pts)

    def tile(h, p, first=0):
        return (
            pl.ds(pl.multiple_of(first + (p // per_row) * 8, 8), 8),
            pl.ds(pl.multiple_of(h * lanes + lax.rem(p, per_row) * cols, 128), cols),
        )

    barrier = pltpu.get_barrier_semaphore()
    for o in range(1, n_hrs):
        pl.semaphore_signal(barrier, inc=1, device_id=(pts, peer_hrs(o)), device_id_type=pl.DeviceIdType.MESH)
    for o in range(1, n_pts):
        pl.semaphore_signal(barrier, inc=1, device_id=(peer_pts(o), hrs), device_id_type=pl.DeviceIdType.MESH)
    pl.semaphore_wait(barrier, n_hrs + n_pts - 2)

    started = []

    def send(src, dst, ss, rs, device):
        copy = pltpu.make_async_remote_copy(
            src_ref=src, dst_ref=dst, send_sem=ss, recv_sem=rs,
            device_id=device, device_id_type=pl.DeviceIdType.MESH,
        )
        copy.start()
        started.append(copy)
        return copy

    def along(h):
        return pl.ds(h * lanes, lanes)

    mine = pl.ds(pl.multiple_of(hrs * q, 8), q)
    first, second, third, fourth = [], [], [], []
    for h in range(parts):
        copies = []
        for o in range(1, n_hrs):
            t = peer_hrs(o)
            src = x_ref.at[pl.ds(pl.multiple_of(t * q, 8), q), along(h)]
            copies.append(send(src, got1.at[h, o - 1], s1.at[h, o - 1], r1.at[h, o - 1], (pts, t)))
        first.append(copies)
    for h in range(parts):
        total = x_ref[mine, along(h)]
        for o, copy in enumerate(first[h]):
            copy.wait_recv()
            total = total + got1[h, o]
        part[:, along(h)] = total
        copies = []
        for o in range(1, n_pts):
            t = peer_pts(o)
            copies.append(send(part.at[tile(h, t)], got2.at[h, o - 1], s2.at[h, o - 1], r2.at[h, o - 1], (t, hrs)))
        second.append(copies)
    for h in range(parts):
        total = part[tile(h, pts)]
        for o, copy in enumerate(second[h]):
            copy.wait_recv()
            total = total + got2[h, o]
        own = tile(h, pts, hrs * q)
        out_ref[own] = total
        copies = []
        for o in range(1, n_pts):
            t = peer_pts(o)
            copies.append(send(out_ref.at[own], out_ref.at[own], s3.at[h, o - 1], r3.at[h, o - 1], (t, hrs)))
        third.append(copies)
    for h in range(parts):
        for copy in third[h]:
            copy.wait_recv()
        copies = []
        block = out_ref.at[mine, along(h)]
        for o in range(1, n_hrs):
            copies.append(send(block, block, s4.at[h, o - 1], r4.at[h, o - 1], (pts, peer_hrs(o))))
        fourth.append(copies)
    for copies in fourth:
        for copy in copies:
            copy.wait_recv()
    for copy in started:
        copy.wait_send()


def sum_all(x, n_pts, n_hrs, parts=2):
    rows, width = x.shape
    q = rows // n_hrs
    parts = max(1, min(parts, q * width // (8 * 128 * n_pts)))
    lanes = width // parts
    cols = q * lanes // (8 * n_pts)
    v = pl.BlockSpec(memory_space=pltpu.VMEM)
    dma = pltpu.SemaphoreType.DMA
    return pl.pallas_call(
        functools.partial(sum_kernel, n_pts, n_hrs, lanes, cols),
        out_shape=jax.ShapeDtypeStruct(x.shape, jnp.float32),
        in_specs=[v],
        out_specs=v,
        scratch_shapes=[
            pltpu.VMEM((parts, n_hrs - 1, q, lanes), jnp.float32),
            pltpu.VMEM((q, width), jnp.float32),
            pltpu.VMEM((parts, n_pts - 1, 8, cols), jnp.float32),
            dma((parts, n_hrs - 1)), dma((parts, n_hrs - 1)),
            dma((parts, n_pts - 1)), dma((parts, n_pts - 1)),
            dma((parts, n_pts - 1)), dma((parts, n_pts - 1)),
            dma((parts, n_hrs - 1)), dma((parts, n_hrs - 1)),
        ],
        compiler_params=pltpu.CompilerParams(collective_id=0, has_side_effects=True),
        name="sum_all",
    )(x)


def gather_kernel(n_pts, n_hrs, chunks, n_points, fields_ref, probes_ref, sk_ref, cross_ref, panels, flat, own_sem, send_sem, recv_sem):
    pts, hrs = lax.axis_index("pts"), lax.axis_index("hrs")
    n = n_pts * n_hrs
    me = pts * n_hrs + hrs
    rows = fields_ref.shape[0]
    width = panels.shape[3]
    local = width * chunks

    def split(o):
        t = lax.rem(me + o, n)
        return t, t // n_hrs, lax.rem(t, n_hrs)

    barrier = pltpu.get_barrier_semaphore()

    @pl.loop(1, n)
    def _(o):
        _, tp, th = split(o)
        pl.semaphore_signal(barrier, inc=1, device_id=(tp, th), device_id_type=pl.DeviceIdType.MESH)

    pl.semaphore_wait(barrier, n - 1)

    def source(t, c):
        return fields_ref.at[:, pl.ds(pl.multiple_of(t * local + c * width, 128), width)]

    owns = []
    for c in range(chunks):
        @pl.loop(1, n)
        def _(o):
            t, tp, th = split(o)
            pltpu.make_async_remote_copy(
                src_ref=source(t, c), dst_ref=panels.at[c, me], send_sem=send_sem.at[c], recv_sem=recv_sem.at[c],
                device_id=(tp, th), device_id_type=pl.DeviceIdType.MESH,
            ).start()

        own = pltpu.make_async_copy(source(me, c), panels.at[c, me], own_sem.at[c])
        own.start()
        owns.append(own)

    for c in range(chunks):
        owns[c].wait()
        most = panels.at[c, pl.ds(0, n - 1)]
        pltpu.make_async_copy(most, most, recv_sem.at[c]).wait()
        if rows % 8 == 0:
            block = panels[c].reshape(n * rows, width)
        else:
            for d in range(n):
                flat[d * rows:(d + 1) * rows, :] = panels[c, d]
            block = flat[...]
        sk = mm(probes_ref[...], block, ((1,), (0,)))
        sk_ref[:, c * width:(c + 1) * width] = sk
        term = mm(sk, block, ((1,), (1,)))
        cross_ref[...] = term if c == 0 else cross_ref[...] + term
    cross_ref[...] = cross_ref[...] / n_points
    for c in range(chunks):
        most = panels.at[c, pl.ds(0, n - 1)]
        pltpu.make_async_copy(most, most, send_sem.at[c]).wait()


def gather(fields, probes, n_pts, n_hrs, chunks):
    k, hours = probes.shape
    rows, n_points = fields.shape
    n = n_pts * n_hrs
    local = n_points // n
    width = local // chunks
    v = pl.BlockSpec(memory_space=pltpu.VMEM)
    dma = pltpu.SemaphoreType.DMA
    return pl.pallas_call(
        functools.partial(gather_kernel, n_pts, n_hrs, chunks, n_points),
        out_shape=(jax.ShapeDtypeStruct((k, local), jnp.float32), jax.ShapeDtypeStruct((k, hours), jnp.float32)),
        in_specs=[pl.BlockSpec(memory_space=pl.ANY), v],
        out_specs=(v, v),
        scratch_shapes=[
            pltpu.VMEM((chunks, n, rows, width), jnp.float32),
            pltpu.VMEM((hours, width) if rows % 8 else (8, 128), jnp.float32),
            dma((chunks,)), dma((chunks,)), dma((chunks,)),
        ],
        compiler_params=pltpu.CompilerParams(collective_id=1, has_side_effects=True),
        name="gather",
    )(fields, probes)


def on_device(fields, probes):
    n_pts = lax.axis_size("pts")
    n_hrs = lax.axis_size("hrs")
    sketched, cross = gather(fields, probes, n_pts, n_hrs, 4)
    return finish(sum_all(cross, n_pts, n_hrs), probes, sketched)


def solution(mesh):
    return jax.shard_map(
        on_device,
        mesh=mesh,
        in_specs=(P(("pts", "hrs"), None), P()),
        out_specs=(P(None, ("pts", "hrs")), P()),
        check_vma=False,
    )
```

profile of v0, /device:TPU:0, one launch (start us, length us, event | category | flops | bytes accessed | tf_op | source)
XLA Modules:
  0.0 146.2 jit_solution(8982425043035844869)
XLA Ops:
  0.6 94.5 %gather.1 = (f32[256,2048]{1,0:T(8,128)}, f32[256,512]{1,0:T(8,128)}) custom-call(f32[16,65536]{1,0:T(8,128)} %fields_ref.1, f32[256,512]{1,0:T(8,128)} %probes_ref.3), custom_call_target="tpu_custom_call" | custom-call | tf_op jit(solution)/shard_map/gather/pallas_call | solution.py:279
  95.2 33.7 %sum_all.1.cross_ref = f32[256,512]{1,0:T(8,128)} custom-call(f32[256,512]{1,0:T(8,128)} %get-tuple-element.4.x_ref), custom_call_target="tpu_custom_call" | custom-call | tf_op jit(solution)/shard_map/sum_all/pallas_call | solution.py:194
  128.9 17.4 %factor.1 = (f32[256,2048]{1,0:T(8,128)}, f32[256,512]{1,0:T(8,128)}) custom-call(f32[256,512]{1,0:T(8,128)} %sum_all.1.cross_ref, f32[256,512]{1,0:T(8,128)} %probes_ref.3, f32[256,2048]{1,0:T(8,128)} %get-tuple-element.5.sk_ref), custom_call_target="tpu_custom_call" | custom-call | tf_op jit(solution)/shard_map/factor/pallas_call | solution.py:92
where the time goes:
time: 146 us
  Pallas kernels  146 us (100%)
    pallas_call x1, Pallas kernels, gather(): pl.pallas_call(functools.partial(gather_kernel, n_pts, n_hrs, chunks, n_p...  94.5 us
    pallas_call x1, Pallas kernels, sum_all(): pl.pallas_call(functools.partial(sum_kernel, n_pts, n_hrs, lanes, cols),...  33.7 us
    pallas_call x1, Pallas kernels, finish(): pl.pallas_call(factor_kernel, out_shape=(jax.ShapeDtypeStruct(sk.shape, j...  17.4 us

commit v1 on v0

v1 whole, which is shorter than its diff:
```python
import functools

import jax
import jax.numpy as jnp
from jax import lax
from jax.experimental import pallas as pl
from jax.experimental.pallas import tpu as pltpu
from jax.sharding import PartitionSpec as P

HI = lax.Precision.HIGHEST
MESH = pl.DeviceIdType.MESH


def mm(a, b, dims):
    return lax.dot_general(a, b, (dims, ((), ())), precision=HI, preferred_element_type=jnp.float32)


def invert_block(block):
    b = block.shape[0]
    n = b // 8
    shape = (8, b)
    srow = lax.broadcasted_iota(jnp.int32, shape, 0)
    lane = lax.broadcasted_iota(jnp.int32, shape, 1)
    strips = [block[8 * s:8 * s + 8] for s in range(n)]
    diag = sum(jnp.where(lane == srow + 8 * s, strips[s], 0.0) for s in range(n))
    diag = jnp.broadcast_to(jnp.sum(diag, axis=0, keepdims=True), shape)
    col = 1.0 / diag
    root = lax.rsqrt(diag)
    strips = [strip * col for strip in strips]
    outs = [jnp.zeros(shape, jnp.float32)] * n

    def row_of(x, r):
        return jnp.broadcast_to(x[r:r + 1], shape)

    def spread(x, c, apart=True):
        x = jnp.broadcast_to(x[:, c:c + 1], shape)
        return jnp.maximum(x, -3e38) if apart else x

    for s0 in range(n):
        j = 8 * s0
        panel = {s: [spread(strips[s], j + c, s == s0) for c in range(8)] for s in range(s0, n)}
        roots = [spread(root, j + c) for c in range(8)]
        inside = (lane >= j) & (lane < j + 8)
        for s in range(s0, n):
            unit = jnp.where(lane == srow + j, 1.0, 0.0) if s == s0 else 0.0
            strips[s] = jnp.where(inside, unit, strips[s])
        head = panel[s0]
        for p in range(0, 8, 2):
            a, b12 = row_of(head[p], p), row_of(head[p + 1], p)
            b21, c = row_of(head[p], p + 1), row_of(head[p + 1], p + 1)
            det = a * c - b12 * b21
            inv = 1.0 / det
            inva = 1.0 / a
            row1, row2 = row_of(strips[s0], p), row_of(strips[s0], p + 1)
            w1 = row1 * (lax.rsqrt(a) * roots[p])
            w2 = (row2 - (b21 * inva) * row1) * (lax.rsqrt(det * inva) * roots[p + 1])
            outs[s0] = jnp.where(srow == p, w1, jnp.where(srow == p + 1, w2, outs[s0]))
            v1, v2 = (c * row1 - b12 * row2) * inv, (a * row2 - b21 * row1) * inv
            y = {}
            for q in range(p + 2, 8):
                e1, e2 = row_of(head[q], p), row_of(head[q], p + 1)
                y[q] = (c * e1 - b12 * e2, a * e2 - b21 * e1)
            z = {q: (y[q][0] * inv, y[q][1] * inv) for q in y}
            for s in range(s0 if p < 6 else s0 + 1, n):
                f = panel[s]
                for q in range(p + 2, 8):
                    if s < s0 + 2:
                        f[q] = f[q] - (f[p] * y[q][0] + f[p + 1] * y[q][1]) * inv
                    else:
                        f[q] = f[q] - f[p] * z[q][0] - f[p + 1] * z[q][1]
                strips[s] = strips[s] - f[p] * v1 - f[p + 1] * v2
    return jnp.concatenate([jnp.where(lane <= srow + 8 * s, outs[s], 0.0) for s in range(n)], axis=0)


def factor(a, w, b):
    k = a.shape[0]
    for lo in range(0, k, b):
        hi = lo + b
        d = invert_block(a[lo:hi, lo:hi])
        if hi < k:
            lt = mm(d, a[lo:hi, hi:], ((1,), (0,)))
            a[hi:, hi:] = a[hi:, hi:] - mm(lt, lt, ((0,), (0,)))
            w[lo:hi, hi:] = jnp.zeros((b, k - hi), jnp.float32)
        w[lo:hi, lo:hi] = d
        if lo:
            w[lo:hi, :lo] = mm(d, w[lo:hi, :lo], ((1,), (0,)))
        if hi < k:
            t = mm(lt, w[lo:hi, :hi], ((0,), (0,)))
            if lo:
                w[hi:, :lo] = w[hi:, :lo] - t[:, :lo]
            w[hi:, lo:hi] = -t[:, lo:]


def finish_kernel(cross, probes, sk_hbm, basis, coeffs, gram, w, sk, y, sk_sem, out_sem):
    k = gram.shape[0]
    half = k // 2
    n = sk.shape[1]
    load = pltpu.make_async_copy(sk_hbm, sk, sk_sem)
    load.start()
    gram[...] = mm(cross[...], probes[...], ((1,), (1,)))
    factor(gram, w, half)
    load.wait()
    stores = []
    for i, (lo, hi) in enumerate(((0, half), (half, k))):
        for t in range(0, n, 512):
            y[lo:hi, t:t + 512] = mm(w[lo:hi, :hi], sk[:hi, t:t + 512], ((1,), (0,)))
        stores.append(pltpu.make_async_copy(y.at[lo:hi], basis.at[lo:hi], out_sem.at[i]))
        stores[-1].start()
        coeffs[lo:hi, :] = mm(w[lo:hi, :hi], cross[:hi, :], ((1,), (0,)))
    for store in stores:
        store.wait()


def finish(cross, probes, sk):
    k = cross.shape[0]
    v = pl.BlockSpec(memory_space=pltpu.VMEM)
    hbm = pl.BlockSpec(memory_space=pl.ANY)
    f32 = jnp.float32
    return pl.pallas_call(
        finish_kernel,
        out_shape=(jax.ShapeDtypeStruct(sk.shape, f32), jax.ShapeDtypeStruct(cross.shape, f32)),
        in_specs=[v, v, hbm],
        out_specs=(hbm, v),
        scratch_shapes=[
            pltpu.VMEM((k, k), f32), pltpu.VMEM((k, k), f32), pltpu.VMEM(sk.shape, f32), pltpu.VMEM(sk.shape, f32),
            pltpu.SemaphoreType.DMA(()), pltpu.SemaphoreType.DMA((2,)),
        ],
        name="factor",
    )(cross, probes, sk)


class Place:
    def __init__(self, n_pts, n_hrs):
        self.pts, self.hrs = lax.axis_index("pts"), lax.axis_index("hrs")
        self.n_pts, self.n_hrs = n_pts, n_hrs
        self.cores, self.low, self.chips, self.layers = split(n_pts, n_hrs)
        self.core = lax.rem(self.hrs, self.cores)
        self.layer = self.pts // self.low
        self.chip = (self.hrs // self.cores) * self.low + lax.rem(self.pts, self.low)

    def at(self, core, chip, layer):
        return (layer * self.low + lax.rem(chip, self.low), (chip // self.low) * self.cores + core)


def split(n_pts, n_hrs):
    cores = 2 if n_hrs % 2 == 0 else 1
    low = 1
    while n_pts % (low * 2) == 0 and low * 2 * low * 2 <= n_pts:
        low *= 2
    return cores, low, (n_hrs // cores) * low, n_pts // low


def reduce_shapes(n_pts, n_hrs, rows, width, parts):
    cores, low, chips, layers = split(n_pts, n_hrs)
    lanes = width // cores
    h = rows // parts
    q = h // chips
    f32 = jnp.float32
    dma = pltpu.SemaphoreType.DMA
    return [
        pltpu.VMEM((parts, h, lanes), f32),
        pltpu.VMEM((parts, h, lanes), f32),
        pltpu.VMEM((parts, max(chips - 1, 1), q, lanes), f32),
        pltpu.VMEM((parts, layers, q, lanes), f32),
        dma((parts, 2)), dma((parts, 2)),
        dma((parts, 2, max(chips - 1, 1))), dma((parts, 2, max(chips - 1, 1))),
        dma((parts, max(layers - 1, 1))), dma((parts, max(layers - 1, 1))),
    ]


class AllReduce:
    def __init__(self, place, x, out, parts, scale, scratch):
        self.place, self.x, self.out, self.parts, self.scale = place, x, out, parts, scale
        self.got1, self.sum1, self.got2, self.sums, self.s1, self.r1, self.s2, self.r2, self.s3, self.r3 = scratch
        self.h, self.lanes = self.got1.shape[1], self.got1.shape[2]
        self.q = self.sums.shape[2]
        self.started = []
        self.copies = {}

    def send(self, key, src, dst, ss, rs, device):
        copy = pltpu.make_async_remote_copy(
            src_ref=src, dst_ref=dst, send_sem=ss, recv_sem=rs, device_id=device, device_id_type=MESH)
        copy.start()
        self.started.append(copy)
        self.copies.setdefault(key, []).append(copy)

    def arrived(self, key):
        for copy in self.copies.get(key, ()):
            copy.wait_recv()

    def half(self, core, p):
        return pl.ds(p * self.h, self.h), pl.ds(pl.multiple_of(core * self.lanes, 128), self.lanes)

    def piece(self, chip):
        return pl.ds(pl.multiple_of(chip * self.q, 8), self.q)

    def cores(self, p):
        at = self.place
        if at.cores > 1:
            other = 1 - at.core
            self.send((1, p), self.x.at[self.half(other, p)], self.got1.at[p], self.s1.at[p, 0], self.r1.at[p, 0],
                      at.at(other, at.chip, at.layer))

    def chips(self, p):
        at = self.place
        self.arrived((1, p))
        mine = self.x[self.half(at.core, p)]
        self.sum1[p] = mine + self.got1[p] if at.cores > 1 else mine
        for o in range(1, at.chips):
            chip = lax.rem(at.chip + o, at.chips)
            self.send((2, p), self.sum1.at[p, self.piece(chip)], self.got2.at[p, o - 1], self.s2.at[p, 0, o - 1], self.r2.at[p, 0, o - 1],
                      at.at(at.core, chip, at.layer))

    def layers(self, p):
        at = self.place
        self.arrived((2, p))
        total = self.sum1[p, self.piece(at.chip)]
        for o in range(1, at.chips):
            total = total + self.got2[p, o - 1]
        self.sums[p, at.layer] = total
        for o in range(1, at.layers):
            layer = lax.rem(at.layer + o, at.layers)
            self.send((3, p), self.sums.at[p, at.layer], self.sums.at[p, at.layer], self.s3.at[p, o - 1], self.r3.at[p, o - 1],
                      at.at(at.core, at.chip, layer))

    def spread(self, p):
        at = self.place
        self.arrived((3, p))
        total = self.sums[p, 0]
        for layer in range(1, at.layers):
            total = total + self.sums[p, layer]
        rows, lanes = self.half(at.core, p)
        block = (pl.ds(pl.multiple_of(p * self.h + at.chip * self.q, 8), self.q), lanes)
        self.out[block] = total * self.scale
        for o in range(1, at.chips):
            chip = lax.rem(at.chip + o, at.chips)
            self.send((4, p), self.out.at[block], self.out.at[block], self.s2.at[p, 1, o - 1], self.r2.at[p, 1, o - 1],
                      at.at(at.core, chip, at.layer))

    def share(self, p):
        at = self.place
        self.arrived((4, p))
        if at.cores > 1:
            half = self.half(at.core, p)
            self.send((5, p), self.out.at[half], self.out.at[half], self.s1.at[p, 1], self.r1.at[p, 1],
                      at.at(1 - at.core, at.chip, at.layer))

    def run(self, step):
        for p in range(self.parts):
            step(p)

    def finish(self):
        for p in range(self.parts):
            self.arrived((5, p))

    def drain(self):
        for copy in self.started:
            copy.wait_send()


def gather_kernel(n_pts, n_hrs, widths, parts, n_points, fields_ref, probes_ref, sk_hbm, cross_ref, *scratch):
    n = n_pts * n_hrs
    m = len(widths)
    panels, scratch = scratch[:m], scratch[m:]
    flat, part, sk, own_sem, send_sem, recv_sem, sk_sem, *scratch = scratch
    place = Place(n_pts, n_hrs)
    me = place.pts * n_hrs + place.hrs
    rows = fields_ref.shape[0]
    local = sum(widths)
    k, hours = part.shape

    def split_id(o):
        t = lax.rem(me + o, n)
        return t, t // n_hrs, lax.rem(t, n_hrs)

    barrier = pltpu.get_barrier_semaphore()

    @pl.loop(1, n)
    def _(o):
        _, tp, th = split_id(o)
        pl.semaphore_signal(barrier, inc=1, device_id=(tp, th), device_id_type=MESH)

    pl.semaphore_wait(barrier, n - 1)

    starts = [sum(widths[:c]) for c in range(m)]

    def source(t, c):
        return fields_ref.at[:, pl.ds(pl.multiple_of(t * local + starts[c], 128), widths[c])]

    owns = []
    for c in range(m):
        @pl.loop(1, n)
        def _(o):
            t, tp, th = split_id(o)
            pltpu.make_async_remote_copy(
                src_ref=source(t, c), dst_ref=panels[c].at[me], send_sem=send_sem.at[c], recv_sem=recv_sem.at[c],
                device_id=(tp, th), device_id_type=MESH,
            ).start()

        own = pltpu.make_async_copy(source(me, c), panels[c].at[me], own_sem.at[c])
        own.start()
        owns.append(own)

    reduce = AllReduce(place, part, cross_ref, parts, 1.0 / n_points, scratch)
    stores = []
    for c in range(m):
        owns[c].wait()
        most = panels[c].at[pl.ds(0, n - 1)]
        pltpu.make_async_copy(most, most, recv_sem.at[c]).wait()
        width = widths[c]
        cols = pl.ds(starts[c], width)
        if rows % 8 == 0:
            block = panels[c][...].reshape(n * rows, width)
        else:
            for d in range(n):
                flat[d * rows:(d + 1) * rows, :width] = panels[c][d]
            block = flat[:, :width]
        sk[:, cols] = mm(probes_ref[...], block, ((1,), (0,)))
        term = mm(sk[:, cols], block, ((1,), (1,)))
        part[...] = term if c == 0 else part[...] + term
        stores.append(pltpu.make_async_copy(sk.at[:, cols], sk_hbm.at[:, cols], sk_sem.at[c]))
        if c < m - 1:
            stores[-1].start()
    reduce.run(reduce.cores)
    stores[-1].start()
    reduce.run(reduce.chips)
    reduce.run(reduce.layers)
    reduce.run(reduce.spread)
    reduce.run(reduce.share)
    reduce.finish()
    reduce.drain()
    for store in stores:
        store.wait()
    for c in range(m):
        most = panels[c].at[pl.ds(0, n - 1)]
        pltpu.make_async_copy(most, most, send_sem.at[c]).wait()


def gather(fields, probes, n_pts, n_hrs):
    k, hours = probes.shape
    rows, n_points = fields.shape
    n = n_pts * n_hrs
    local = n_points // n
    widths = pieces(local)
    m = len(widths)
    cores, low, chips, layers = split(n_pts, n_hrs)
    parts = 2 if k % (2 * chips * 8) == 0 else 1
    v = pl.BlockSpec(memory_space=pltpu.VMEM)
    hbm = pl.BlockSpec(memory_space=pl.ANY)
    dma = pltpu.SemaphoreType.DMA
    f32 = jnp.float32
    return pl.pallas_call(
        functools.partial(gather_kernel, n_pts, n_hrs, widths, parts, n_points),
        out_shape=(jax.ShapeDtypeStruct((k, local), f32), jax.ShapeDtypeStruct((k, hours), f32)),
        in_specs=[hbm, v],
        out_specs=(hbm, v),
        scratch_shapes=[
            *(pltpu.VMEM((n, rows, width), f32) for width in widths),
            pltpu.VMEM((hours, max(widths)) if rows % 8 else (8, 128), f32),
            pltpu.VMEM((k, hours), f32),
            pltpu.VMEM((k, local), f32),
            dma((m,)), dma((m,)), dma((m,)), dma((m,)),
            *reduce_shapes(n_pts, n_hrs, k, hours, parts),
        ],
        compiler_params=pltpu.CompilerParams(collective_id=1, has_side_effects=True),
        name="gather",
    )(fields, probes)


def pieces(local):
    if local % 128 or local < 1024:
        return (local,)
    last = 128
    big = 512
    rest = local - last
    widths = []
    while rest > big:
        widths.append(big)
        rest -= big
    return (*widths, rest, last)


def on_device(fields, probes):
    n_pts = lax.axis_size("pts")
    n_hrs = lax.axis_size("hrs")
    sketched, cross = gather(fields, probes, n_pts, n_hrs)
    return finish(cross, probes, sketched)


def solution(mesh):
    return jax.shard_map(
        on_device,
        mesh=mesh,
        in_specs=(P(("pts", "hrs"), None), P()),
        out_specs=(P(None, ("pts", "hrs")), P()),
        check_vma=False,
    )
```

time: 146 us -> 132 us (0.904)
  Pallas kernels: 146 us -> 131 us
    pallas_call x3 -> x2, Pallas kernels: 146 us -> 131 us  [the longest x1 119 us: gather(): pl.pallas_call(functools.partial(gather_kernel, n_pts, n_hrs, widths, par...]
where the time goes in v1:
time: 132 us
  Pallas kernels  131 us (99%)
    pallas_call x1, Pallas kernels, gather(): pl.pallas_call(functools.partial(gather_kernel, n_pts, n_hrs, widths, par...  119 us
    pallas_call x1, Pallas kernels, finish(): pl.pallas_call(finish_kernel, out_shape=(jax.ShapeDtypeStruct(sk.shape, f...  12.5 us

profile of v1, /device:TPU:0, one launch (start us, length us, event | category | flops | bytes accessed | tf_op | source)
XLA Modules:
  0.0 132.0 jit_solution(13836577449813013958)
XLA Ops:
  0.6 118.8 %gather.1 = (f32[256,2048]{1,0:T(8,128)}, f32[256,512]{1,0:T(8,128)}) custom-call(f32[16,65536]{1,0:T(8,128)} %fields_ref.1, f32[256,512]{1,0:T(8,128)} %probes.1), custom_call_target="tpu_custom_call" | custom-call | tf_op jit(solution)/shard_map/gather/pallas_call | solution.py:352
  119.4 12.5 %factor.1 = (f32[256,2048]{1,0:T(8,128)}, f32[256,512]{1,0:T(8,128)}) custom-call(f32[256,512]{1,0:T(8,128)} %get-tuple-element.4.cross, f32[256,512]{1,0:T(8,128)} %probes.1, f32[256,2048]{1,0:T(8,128)} %get-tuple-element.5.sk_hbm), custom_call_target="tpu_custom_call" | custom-call | tf_op jit(solution)/shard_map/factor/pallas_call | solution.py:119

commit v2 on v1

--- a/solution.py
+++ b/solution.py
@@ -9,13 +9,14 @@
 
 HI = lax.Precision.HIGHEST
 MESH = pl.DeviceIdType.MESH
+POINTS = ((0, 0), (0, 6), (1, 2), (1, 13))
 
 
 def mm(a, b, dims):
     return lax.dot_general(a, b, (dims, ((), ())), precision=HI, preferred_element_type=jnp.float32)
 
 
-def invert_block(block):
+def invert_block(block, between=None):
     b = block.shape[0]
     n = b // 8
     shape = (8, b)
@@ -38,6 +39,8 @@
 
     for s0 in range(n):
         j = 8 * s0
+        if between is not None:
+            between(s0)
         panel = {s: [spread(strips[s], j + c, s == s0) for c in range(8)] for s in range(s0, n)}
         roots = [spread(root, j + c) for c in range(8)]
         inside = (lane >= j) & (lane < j + 8)
@@ -72,61 +75,72 @@
     return jnp.concatenate([jnp.where(lane <= srow + 8 * s, outs[s], 0.0) for s in range(n)], axis=0)
 
 
-def factor(a, w, b):
-    k = a.shape[0]
-    for lo in range(0, k, b):
-        hi = lo + b
-        d = invert_block(a[lo:hi, lo:hi])
-        if hi < k:
-            lt = mm(d, a[lo:hi, hi:], ((1,), (0,)))
-            a[hi:, hi:] = a[hi:, hi:] - mm(lt, lt, ((0,), (0,)))
-            w[lo:hi, hi:] = jnp.zeros((b, k - hi), jnp.float32)
-        w[lo:hi, lo:hi] = d
-        if lo:
-            w[lo:hi, :lo] = mm(d, w[lo:hi, :lo], ((1,), (0,)))
-        if hi < k:
-            t = mm(lt, w[lo:hi, :hi], ((0,), (0,)))
-            if lo:
-                w[hi:, :lo] = w[hi:, :lo] - t[:, :lo]
-            w[hi:, lo:hi] = -t[:, lo:]
-
-
-def finish_kernel(cross, probes, sk_hbm, basis, coeffs, gram, w, sk, y, sk_sem, out_sem):
-    k = gram.shape[0]
-    half = k // 2
+def packed(k, chips, parts):
+    step = 8 * chips * parts
+    return -(-(k // 2 + k // 4) // step) * step
+
+
+def pack(g, gram, first):
+    k = gram.shape[1]
+    h, q = k // 2, k // 4
+    for rows, cols, block in (
+        (slice(0, h), slice(0, h), g[:h, :h]),
+        (slice(0, h), slice(h, k), g[h:, h:]),
+        (slice(h, h + q), slice(0, h), g[h:h + q, :h]),
+        (slice(h, h + q), slice(h, k), g[h + q:, :h]),
+    ):
+        gram[rows, cols] = block if first else gram[rows, cols] + block
+
+
+def factor(gram, w, between):
+    k = w.shape[0]
+    h, q = k // 2, k // 4
+    top = invert_block(gram[:h, :h], functools.partial(between, 0))
+    w[:h, :h] = top
+    w[:h, h:] = jnp.zeros((h, k - h), jnp.float32)
+    below = jnp.concatenate([gram[h:h + q, :h], gram[h:h + q, h:]], axis=0)
+    side = mm(below, top, ((1,), (1,)))
+    rest = gram[:h, h:] - mm(side, side, ((1,), (1,)))
+    w[h:, :h] = mm(side, top, ((1,), (0,)))
+    last = invert_block(rest, functools.partial(between, 1))
+    w[h:, h:] = last
+    w[h:, :h] = -mm(last, w[h:, :h], ((1,), (0,)))
+
+
+def apply_kernel(w, cross, sk_hbm, basis, coeffs, sk, y, sk_sem, out_sem):
     n = sk.shape[1]
-    load = pltpu.make_async_copy(sk_hbm, sk, sk_sem)
-    load.start()
-    gram[...] = mm(cross[...], probes[...], ((1,), (1,)))
-    factor(gram, w, half)
-    load.wait()
-    stores = []
-    for i, (lo, hi) in enumerate(((0, half), (half, k))):
-        for t in range(0, n, 512):
-            y[lo:hi, t:t + 512] = mm(w[lo:hi, :hi], sk[:hi, t:t + 512], ((1,), (0,)))
-        stores.append(pltpu.make_async_copy(y.at[lo:hi], basis.at[lo:hi], out_sem.at[i]))
+    step = 512
+    loads, stores = [], []
+    for t in range(0, n, step):
+        loads.append(pltpu.make_async_copy(sk_hbm.at[:, t:t + step], sk.at[:, t:t + step], sk_sem.at[len(loads)]))
+        loads[-1].start()
+    for i, t in enumerate(range(0, n, step)):
+        loads[i].wait()
+        y[:, t:t + step] = mm(w[...], sk[:, t:t + step], ((1,), (0,)))
+        stores.append(pltpu.make_async_copy(y.at[:, t:t + step], basis.at[:, t:t + step], out_sem.at[i]))
         stores[-1].start()
-        coeffs[lo:hi, :] = mm(w[lo:hi, :hi], cross[:hi, :], ((1,), (0,)))
+        if i == 0:
+            coeffs[...] = mm(w[...], cross[...], ((1,), (0,)))
     for store in stores:
         store.wait()
 
 
-def finish(cross, probes, sk):
-    k = cross.shape[0]
+def finish(w, cross, sk):
     v = pl.BlockSpec(memory_space=pltpu.VMEM)
     hbm = pl.BlockSpec(memory_space=pl.ANY)
     f32 = jnp.float32
+    count = -(-sk.shape[1] // 512)
     return pl.pallas_call(
-        finish_kernel,
+        apply_kernel,
         out_shape=(jax.ShapeDtypeStruct(sk.shape, f32), jax.ShapeDtypeStruct(cross.shape, f32)),
         in_specs=[v, v, hbm],
         out_specs=(hbm, v),
         scratch_shapes=[
-            pltpu.VMEM((k, k), f32), pltpu.VMEM((k, k), f32), pltpu.VMEM(sk.shape, f32), pltpu.VMEM(sk.shape, f32),
-            pltpu.SemaphoreType.DMA(()), pltpu.SemaphoreType.DMA((2,)),
+            pltpu.VMEM(sk.shape, f32), pltpu.VMEM(sk.shape, f32),
+            pltpu.SemaphoreType.DMA((count,)), pltpu.SemaphoreType.DMA((count,)),
         ],
-        name="factor",
-    )(cross, probes, sk)
+        name="apply",
+    )(w, cross, sk)
 
 
 class Place:
@@ -258,11 +272,11 @@
             copy.wait_send()
 
 
-def gather_kernel(n_pts, n_hrs, widths, parts, n_points, fields_ref, probes_ref, sk_hbm, cross_ref, *scratch):
+def gather_kernel(n_pts, n_hrs, widths, parts, n_points, fields_ref, probes_ref, sk_hbm, w_ref, cross_ref, *scratch):
     n = n_pts * n_hrs
     m = len(widths)
     panels, scratch = scratch[:m], scratch[m:]
-    flat, part, sk, own_sem, send_sem, recv_sem, sk_sem, *scratch = scratch
+    flat, part, gram, summed, sk, own_sem, send_sem, recv_sem, sk_sem, *scratch = scratch
     place = Place(n_pts, n_hrs)
     me = place.pts * n_hrs + place.hrs
     rows = fields_ref.shape[0]
@@ -301,7 +315,10 @@
         own.start()
         owns.append(own)
 
-    reduce = AllReduce(place, part, cross_ref, parts, 1.0 / n_points, scratch)
+    grams = AllReduce(place, gram, summed, parts, 1.0 / n_points, scratch[:10])
+    crosses = AllReduce(place, part, cross_ref, parts, 1.0 / n_points, scratch[10:])
+    if gram.shape[0] > k // 2 + k // 4:
+        gram[k // 2 + k // 4:, :] = jnp.zeros((gram.shape[0] - k // 2 - k // 4, k), jnp.float32)
     stores = []
     for c in range(m):
         owns[c].wait()
@@ -315,20 +332,33 @@
             for d in range(n):
                 flat[d * rows:(d + 1) * rows, :width] = panels[c][d]
             block = flat[:, :width]
-        sk[:, cols] = mm(probes_ref[...], block, ((1,), (0,)))
-        term = mm(sk[:, cols], block, ((1,), (1,)))
+        sketch = mm(probes_ref[...], block, ((1,), (0,)))
+        sk[:, cols] = sketch
+        pack(mm(sketch, sketch, ((1,), (1,))), gram, c == 0)
+        if c == m - 1:
+            grams.run(grams.cores)
+        term = mm(sketch, block, ((1,), (1,)))
         part[...] = term if c == 0 else part[...] + term
         stores.append(pltpu.make_async_copy(sk.at[:, cols], sk_hbm.at[:, cols], sk_sem.at[c]))
-        if c < m - 1:
-            stores[-1].start()
-    reduce.run(reduce.cores)
-    stores[-1].start()
-    reduce.run(reduce.chips)
-    reduce.run(reduce.layers)
-    reduce.run(reduce.spread)
-    reduce.run(reduce.share)
-    reduce.finish()
-    reduce.drain()
+        stores[-1].start()
+    crosses.run(crosses.cores)
+    grams.run(grams.chips)
+    crosses.run(crosses.chips)
+    grams.run(grams.layers)
+    crosses.run(crosses.layers)
+    grams.run(grams.spread)
+    grams.run(grams.share)
+    grams.finish()
+    todo = {POINTS[p]: functools.partial(step, p % parts) for p, step in enumerate([crosses.spread] * parts + [crosses.share] * parts)}
+
+    def between(block, panel):
+        if (block, panel) in todo:
+            todo[block, panel]()
+
+    factor(summed, w_ref, between)
+    crosses.finish()
+    grams.drain()
+    crosses.drain()
     for store in stores:
         store.wait()
     for c in range(m):
@@ -345,21 +375,27 @@
     m = len(widths)
     cores, low, chips, layers = split(n_pts, n_hrs)
     parts = 2 if k % (2 * chips * 8) == 0 else 1
+    gram_rows = packed(k, chips, parts)
     v = pl.BlockSpec(memory_space=pltpu.VMEM)
     hbm = pl.BlockSpec(memory_space=pl.ANY)
     dma = pltpu.SemaphoreType.DMA
     f32 = jnp.float32
     return pl.pallas_call(
         functools.partial(gather_kernel, n_pts, n_hrs, widths, parts, n_points),
-        out_shape=(jax.ShapeDtypeStruct((k, local), f32), jax.ShapeDtypeStruct((k, hours), f32)),
+        out_shape=(
+            jax.ShapeDtypeStruct((k, local), f32), jax.ShapeDtypeStruct((k, k), f32), jax.ShapeDtypeStruct((k, hours), f32),
+        ),
         in_specs=[hbm, v],
-        out_specs=(hbm, v),
+        out_specs=(hbm, v, v),
         scratch_shapes=[
             *(pltpu.VMEM((n, rows, width), f32) for width in widths),
             pltpu.VMEM((hours, max(widths)) if rows % 8 else (8, 128), f32),
             pltpu.VMEM((k, hours), f32),
+            pltpu.VMEM((gram_rows, k), f32),
+            pltpu.VMEM((gram_rows, k), f32),
             pltpu.VMEM((k, local), f32),
             dma((m,)), dma((m,)), dma((m,)), dma((m,)),
+            *reduce_shapes(n_pts, n_hrs, gram_rows, k, parts),
             *reduce_shapes(n_pts, n_hrs, k, hours, parts),
         ],
         compiler_params=pltpu.CompilerParams(collective_id=1, has_side_effects=True),
@@ -383,8 +419,8 @@
 def on_device(fields, probes):
     n_pts = lax.axis_size("pts")
     n_hrs = lax.axis_size("hrs")
-    sketched, cross = gather(fields, probes, n_pts, n_hrs)
-    return finish(cross, probes, sketched)
+    sketched, w, cross = gather(fields, probes, n_pts, n_hrs)
+    return finish(w, cross, sketched)
 
 
 def solution(mesh):

time: 132 us -> 133 us (level)
    pallas_call x1, Pallas kernels: 119 us -> 125 us  [gather(): pl.pallas_call(functools.partial(gather_kernel, n_pts, n_hrs, widths, par...]
    pallas_call x1, Pallas kernels: 12.5 us -> 6.69 us  [finish(): pl.pallas_call(apply_kernel, out_shape=(jax.ShapeDtypeStruct(sk.shape, f3...]
where the time goes in v2:
time: 133 us; the launch traced here: 132 us
  Pallas kernels  132 us (99%)
    pallas_call x1, Pallas kernels, gather(): pl.pallas_call(functools.partial(gather_kernel, n_pts, n_hrs, widths, par...  125 us
    pallas_call x1, Pallas kernels, finish(): pl.pallas_call(apply_kernel, out_shape=(jax.ShapeDtypeStruct(sk.shape, f3...  6.69 us

profile of v2, /device:TPU:0, one launch (start us, length us, event | category | flops | bytes accessed | tf_op | source)
XLA Modules:
  0.0 132.4 jit_solution(12095480573603422226)
XLA Ops:
  0.6 124.9 %gather.1 = (f32[256,2048]{1,0:T(8,128)}, f32[256,256]{1,0:T(8,128)}, f32[256,512]{1,0:T(8,128)}) custom-call(f32[16,65536]{1,0:T(8,128)} %fields_ref.1, f32[256,512]{1,0:T(8,128)} %probes_ref.1), custom_call_target="tpu_custom_call" | custom-call | tf_op jit(solution)/shard_map/gather/pallas_call | solution.py:383
  125.5 6.7 %apply.1 = (f32[256,2048]{1,0:T(8,128)}, f32[256,512]{1,0:T(8,128)}) custom-call(f32[256,256]{1,0:T(8,128)} %get-tuple-element.5.w, f32[256,512]{1,0:T(8,128)} %get-tuple-element.6.cross, f32[256,2048]{1,0:T(8,128)} %get-tuple-element.7.sk_hbm), custom_call_target="tpu_custom_call" | custom-call | tf_op jit(solution)/shard_map/apply/pallas_call | solution.py:133

commit v3 on v2

--- a/solution.py
+++ b/solution.py
@@ -9,6 +9,7 @@
 
 HI = lax.Precision.HIGHEST
 MESH = pl.DeviceIdType.MESH
+VMEM_LIMIT = 24 * 2 ** 20
 POINTS = ((0, 0), (0, 6), (1, 2), (1, 13))
 
 
@@ -107,20 +108,16 @@
     w[h:, :h] = -mm(last, w[h:, :h], ((1,), (0,)))
 
 
-def apply_kernel(w, cross, sk_hbm, basis, coeffs, sk, y, sk_sem, out_sem):
+def apply_kernel(w, cross, sk, basis, coeffs, y, z, sem):
     n = sk.shape[1]
     step = 512
-    loads, stores = [], []
+    z[...] = mm(w[...], cross[...], ((1,), (0,)))
+    stores = [pltpu.make_async_copy(z, coeffs, sem.at[0])]
+    stores[0].start()
     for t in range(0, n, step):
-        loads.append(pltpu.make_async_copy(sk_hbm.at[:, t:t + step], sk.at[:, t:t + step], sk_sem.at[len(loads)]))
-        loads[-1].start()
-    for i, t in enumerate(range(0, n, step)):
-        loads[i].wait()
         y[:, t:t + step] = mm(w[...], sk[:, t:t + step], ((1,), (0,)))
-        stores.append(pltpu.make_async_copy(y.at[:, t:t + step], basis.at[:, t:t + step], out_sem.at[i]))
+        stores.append(pltpu.make_async_copy(y.at[:, t:t + step], basis.at[:, t:t + step], sem.at[len(stores)]))
         stores[-1].start()
-        if i == 0:
-            coeffs[...] = mm(w[...], cross[...], ((1,), (0,)))
     for store in stores:
         store.wait()
 
@@ -129,16 +126,15 @@
     v = pl.BlockSpec(memory_space=pltpu.VMEM)
     hbm = pl.BlockSpec(memory_space=pl.ANY)
     f32 = jnp.float32
-    count = -(-sk.shape[1] // 512)
     return pl.pallas_call(
         apply_kernel,
         out_shape=(jax.ShapeDtypeStruct(sk.shape, f32), jax.ShapeDtypeStruct(cross.shape, f32)),
-        in_specs=[v, v, hbm],
-        out_specs=(hbm, v),
+        in_specs=[v, v, v],
+        out_specs=(hbm, hbm),
         scratch_shapes=[
-            pltpu.VMEM(sk.shape, f32), pltpu.VMEM(sk.shape, f32),
-            pltpu.SemaphoreType.DMA((count,)), pltpu.SemaphoreType.DMA((count,)),
+            pltpu.VMEM(sk.shape, f32), pltpu.VMEM(cross.shape, f32), pltpu.SemaphoreType.DMA((1 - -sk.shape[1] // 512,)),
         ],
+        compiler_params=pltpu.CompilerParams(vmem_limit_bytes=VMEM_LIMIT),
         name="apply",
     )(w, cross, sk)
 
@@ -272,11 +268,11 @@
             copy.wait_send()
 
 
-def gather_kernel(n_pts, n_hrs, widths, parts, n_points, fields_ref, probes_ref, sk_hbm, w_ref, cross_ref, *scratch):
+def gather_kernel(n_pts, n_hrs, widths, parts, n_points, fields_ref, probes_hbm, sk_hbm, w_ref, cross_ref, *scratch):
     n = n_pts * n_hrs
     m = len(widths)
     panels, scratch = scratch[:m], scratch[m:]
-    flat, part, gram, summed, sk, own_sem, send_sem, recv_sem, sk_sem, *scratch = scratch
+    flat, probes_ref, part, gram, summed, sk, probes_sem, own_sem, send_sem, recv_sem, sk_sem, *scratch = scratch
     place = Place(n_pts, n_hrs)
     me = place.pts * n_hrs + place.hrs
     rows = fields_ref.shape[0]
@@ -287,6 +283,8 @@
         t = lax.rem(me + o, n)
         return t, t // n_hrs, lax.rem(t, n_hrs)
 
+    probes_load = pltpu.make_async_copy(probes_hbm, probes_ref, probes_sem)
+    probes_load.start()
     barrier = pltpu.get_barrier_semaphore()
 
     @pl.loop(1, n)
@@ -320,6 +318,7 @@
     if gram.shape[0] > k // 2 + k // 4:
         gram[k // 2 + k // 4:, :] = jnp.zeros((gram.shape[0] - k // 2 - k // 4, k), jnp.float32)
     stores = []
+    probes_load.wait()
     for c in range(m):
         owns[c].wait()
         most = panels[c].at[pl.ds(0, n - 1)]
@@ -378,6 +377,7 @@
     gram_rows = packed(k, chips, parts)
     v = pl.BlockSpec(memory_space=pltpu.VMEM)
     hbm = pl.BlockSpec(memory_space=pl.ANY)
+    far = pl.BlockSpec(memory_space=pltpu.HBM)
     dma = pltpu.SemaphoreType.DMA
     f32 = jnp.float32
     return pl.pallas_call(
@@ -385,20 +385,21 @@
         out_shape=(
             jax.ShapeDtypeStruct((k, local), f32), jax.ShapeDtypeStruct((k, k), f32), jax.ShapeDtypeStruct((k, hours), f32),
         ),
-        in_specs=[hbm, v],
+        in_specs=[far, far],
         out_specs=(hbm, v, v),
         scratch_shapes=[
             *(pltpu.VMEM((n, rows, width), f32) for width in widths),
             pltpu.VMEM((hours, max(widths)) if rows % 8 else (8, 128), f32),
             pltpu.VMEM((k, hours), f32),
+            pltpu.VMEM((k, hours), f32),
             pltpu.VMEM((gram_rows, k), f32),
             pltpu.VMEM((gram_rows, k), f32),
             pltpu.VMEM((k, local), f32),
-            dma((m,)), dma((m,)), dma((m,)), dma((m,)),
+            dma(()), dma((m,)), dma((m,)), dma((m,)), dma((m,)),
             *reduce_shapes(n_pts, n_hrs, gram_rows, k, parts),
             *reduce_shapes(n_pts, n_hrs, k, hours, parts),
         ],
-        compiler_params=pltpu.CompilerParams(collective_id=1, has_side_effects=True),
+        compiler_params=pltpu.CompilerParams(collective_id=1, has_side_effects=True, vmem_limit_bytes=VMEM_LIMIT),
         name="gather",
     )(fields, probes)
 
@@ -419,7 +420,7 @@
 def on_device(fields, probes):
     n_pts = lax.axis_size("pts")
     n_hrs = lax.axis_size("hrs")
-    sketched, w, cross = gather(fields, probes, n_pts, n_hrs)
+    sketched, w, cross = gather(pltpu.with_memory_space_constraint(fields, pltpu.HBM), pltpu.with_memory_space_constraint(probes, pltpu.HBM), n_pts, n_hrs)
     return finish(w, cross, sketched)
 
 

time: 133 us -> 127 us (0.955)
  Pallas kernels: 132 us -> 126 us
    pallas_call x1, Pallas kernels: 6.69 us -> 3.18 us  [finish(): pl.pallas_call(apply_kernel, out_shape=(jax.ShapeDtypeStruct(sk.shape, f3...]
    pallas_call x1, Pallas kernels: 125 us -> 123 us  [gather(): pl.pallas_call(functools.partial(gather_kernel, n_pts, n_hrs, widths, par...]
where the time goes in v3:
time: 127 us
  Pallas kernels  126 us (99%)
    pallas_call x1, Pallas kernels, gather(): pl.pallas_call(functools.partial(gather_kernel, n_pts, n_hrs, widths, par...  123 us
    pallas_call x1, Pallas kernels, finish(): pl.pallas_call(apply_kernel, out_shape=(jax.ShapeDtypeStruct(sk.shape, f3...  3.18 us

profile of v3, /device:TPU:0, one launch (start us, length us, event | category | flops | bytes accessed | tf_op | source)
XLA Modules:
  0.0 126.8 jit_solution(9449153807700035829)
XLA Ops:
  0.6 122.9 %gather.1 = (f32[256,2048]{1,0:T(8,128)S(1)}, f32[256,256]{1,0:T(8,128)S(1)}, f32[256,512]{1,0:T(8,128)S(1)}) custom-call(f32[16,65536]{1,0:T(8,128)} %fields_ref.1, f32[256,512]{1,0:T(8,128)} %probes_hbm.1), custom_call_target="tpu_custom_call" | custom-call | tf_op jit(solution)/shard_map/gather/pallas_call | solution.py:383
  123.5 3.2 %apply.1 = (f32[256,2048]{1,0:T(8,128)}, f32[256,512]{1,0:T(8,128)}) custom-call(f32[256,256]{1,0:T(8,128)S(1)} %get-tuple-element.5.w, f32[256,512]{1,0:T(8,128)S(1)} %get-tuple-element.6.cross, f32[256,2048]{1,0:T(8,128)S(1)} %get-tuple-element.7.sk), custom_call_target="tpu_custom_call" | custom-call | tf_op jit(solution)/shard_map/apply/pallas_call | solution.py:129

commit v4 on v3

--- a/solution.py
+++ b/solution.py
@@ -8,13 +8,14 @@
 from jax.sharding import PartitionSpec as P
 
 HI = lax.Precision.HIGHEST
+YP = lax.Precision.HIGH
 MESH = pl.DeviceIdType.MESH
 VMEM_LIMIT = 24 * 2 ** 20
-POINTS = ((0, 0), (0, 6), (1, 2), (1, 13))
-
-
-def mm(a, b, dims):
-    return lax.dot_general(a, b, (dims, ((), ())), precision=HI, preferred_element_type=jnp.float32)
+POINTS = ((0, 0), (0, 5), (1, 2), (1, 12))
+
+
+def mm(a, b, dims, precision=HI):
+    return lax.dot_general(a, b, (dims, ((), ())), precision=precision, preferred_element_type=jnp.float32)
 
 
 def invert_block(block, between=None):
@@ -108,35 +109,29 @@
     w[h:, :h] = -mm(last, w[h:, :h], ((1,), (0,)))
 
 
-def apply_kernel(w, cross, sk, basis, coeffs, y, z, sem):
-    n = sk.shape[1]
-    step = 512
+def output_kernel(w, cross, y, basis, coeffs, z, sem):
+    first = pltpu.make_async_copy(y, basis, sem.at[0])
+    first.start()
     z[...] = mm(w[...], cross[...], ((1,), (0,)))
-    stores = [pltpu.make_async_copy(z, coeffs, sem.at[0])]
-    stores[0].start()
-    for t in range(0, n, step):
-        y[:, t:t + step] = mm(w[...], sk[:, t:t + step], ((1,), (0,)))
-        stores.append(pltpu.make_async_copy(y.at[:, t:t + step], basis.at[:, t:t + step], sem.at[len(stores)]))
-        stores[-1].start()
-    for store in stores:
-        store.wait()
-
-
-def finish(w, cross, sk):
+    second = pltpu.make_async_copy(z, coeffs, sem.at[1])
+    second.start()
+    first.wait()
+    second.wait()
+
+
+def finish(w, cross, y):
     v = pl.BlockSpec(memory_space=pltpu.VMEM)
     hbm = pl.BlockSpec(memory_space=pl.ANY)
     f32 = jnp.float32
     return pl.pallas_call(
-        apply_kernel,
-        out_shape=(jax.ShapeDtypeStruct(sk.shape, f32), jax.ShapeDtypeStruct(cross.shape, f32)),
+        output_kernel,
+        out_shape=(jax.ShapeDtypeStruct(y.shape, f32), jax.ShapeDtypeStruct(cross.shape, f32)),
         in_specs=[v, v, v],
         out_specs=(hbm, hbm),
-        scratch_shapes=[
-            pltpu.VMEM(sk.shape, f32), pltpu.VMEM(cross.shape, f32), pltpu.SemaphoreType.DMA((1 - -sk.shape[1] // 512,)),
-        ],
+        scratch_shapes=[pltpu.VMEM(cross.shape, f32), pltpu.SemaphoreType.DMA((2,))],
         compiler_params=pltpu.CompilerParams(vmem_limit_bytes=VMEM_LIMIT),
-        name="apply",
-    )(w, cross, sk)
+        name="output",
+    )(w, cross, y)
 
 
 class Place:
@@ -268,11 +263,11 @@
             copy.wait_send()
 
 
-def gather_kernel(n_pts, n_hrs, widths, parts, n_points, fields_ref, probes_hbm, sk_hbm, w_ref, cross_ref, *scratch):
+def gather_kernel(n_pts, n_hrs, widths, parts, n_points, fields_ref, probes_hbm, y_ref, w_ref, cross_ref, *scratch):
     n = n_pts * n_hrs
     m = len(widths)
     panels, scratch = scratch[:m], scratch[m:]
-    flat, probes_ref, part, gram, summed, sk, probes_sem, own_sem, send_sem, recv_sem, sk_sem, *scratch = scratch
+    flat, probes_ref, part, gram, summed, sk, probes_sem, own_sem, send_sem, recv_sem, *scratch = scratch
     place = Place(n_pts, n_hrs)
     me = place.pts * n_hrs + place.hrs
     rows = fields_ref.shape[0]
@@ -317,7 +312,6 @@
     crosses = AllReduce(place, part, cross_ref, parts, 1.0 / n_points, scratch[10:])
     if gram.shape[0] > k // 2 + k // 4:
         gram[k // 2 + k // 4:, :] = jnp.zeros((gram.shape[0] - k // 2 - k // 4, k), jnp.float32)
-    stores = []
     probes_load.wait()
     for c in range(m):
         owns[c].wait()
@@ -336,11 +330,22 @@
         pack(mm(sketch, sketch, ((1,), (1,))), gram, c == 0)
         if c == m - 1:
             grams.run(grams.cores)
-        term = mm(sketch, block, ((1,), (1,)))
-        part[...] = term if c == 0 else part[...] + term
-        stores.append(pltpu.make_async_copy(sk.at[:, cols], sk_hbm.at[:, cols], sk_sem.at[c]))
-        stores[-1].start()
-    crosses.run(crosses.cores)
+        if c < m - 1:
+            term = mm(sketch, block, ((1,), (1,)))
+            part[...] = term if c == 0 else part[...] + term
+        else:
+            span = n // crosses.place.cores
+            for own in range(crosses.place.cores):
+                core = lax.rem(crosses.place.core + 1 + own, crosses.place.cores)
+                lanes = pl.ds(pl.multiple_of(core * span * rows, 128), span * rows)
+                if rows % 8 == 0:
+                    block = panels[c][pl.ds(core * span, span)].reshape(span * rows, width)
+                else:
+                    block = flat[pl.ds(pl.multiple_of(core * span * rows, 8), span * rows), :width]
+                term = mm(sketch, block, ((1,), (1,)))
+                part[:, lanes] = term if c == 0 else part[:, lanes] + term
+                if own == 0:
+                    crosses.run(crosses.cores)
     grams.run(grams.chips)
     crosses.run(crosses.chips)
     grams.run(grams.layers)
@@ -350,16 +355,18 @@
     grams.finish()
     todo = {POINTS[p]: functools.partial(step, p % parts) for p, step in enumerate([crosses.spread] * parts + [crosses.share] * parts)}
 
+
     def between(block, panel):
         if (block, panel) in todo:
             todo[block, panel]()
 
     factor(summed, w_ref, between)
+    step = 512
+    for t in range(0, local, step):
+        y_ref[:, t:t + step] = mm(w_ref[...], sk[:, t:t + step], ((1,), (0,)), YP)
     crosses.finish()
     grams.drain()
     crosses.drain()
-    for store in stores:
-        store.wait()
     for c in range(m):
         most = panels[c].at[pl.ds(0, n - 1)]
         pltpu.make_async_copy(most, most, send_sem.at[c]).wait()
@@ -376,7 +383,6 @@
     parts = 2 if k % (2 * chips * 8) == 0 else 1
     gram_rows = packed(k, chips, parts)
     v = pl.BlockSpec(memory_space=pltpu.VMEM)
-    hbm = pl.BlockSpec(memory_space=pl.ANY)
     far = pl.BlockSpec(memory_space=pltpu.HBM)
     dma = pltpu.SemaphoreType.DMA
     f32 = jnp.float32
@@ -386,7 +392,7 @@
             jax.ShapeDtypeStruct((k, local), f32), jax.ShapeDtypeStruct((k, k), f32), jax.ShapeDtypeStruct((k, hours), f32),
         ),
         in_specs=[far, far],
-        out_specs=(hbm, v, v),
+        out_specs=(v, v, v),
         scratch_shapes=[
             *(pltpu.VMEM((n, rows, width), f32) for width in widths),
             pltpu.VMEM((hours, max(widths)) if rows % 8 else (8, 128), f32),
@@ -395,7 +401,7 @@
             pltpu.VMEM((gram_rows, k), f32),
             pltpu.VMEM((gram_rows, k), f32),
             pltpu.VMEM((k, local), f32),
-            dma(()), dma((m,)), dma((m,)), dma((m,)), dma((m,)),
+            dma(()), dma((m,)), dma((m,)), dma((m,)),
             *reduce_shapes(n_pts, n_hrs, gram_rows, k, parts),
             *reduce_shapes(n_pts, n_hrs, k, hours, parts),
         ],
@@ -420,8 +426,8 @@
 def on_device(fields, probes):
     n_pts = lax.axis_size("pts")
     n_hrs = lax.axis_size("hrs")
-    sketched, w, cross = gather(pltpu.with_memory_space_constraint(fields, pltpu.HBM), pltpu.with_memory_space_constraint(probes, pltpu.HBM), n_pts, n_hrs)
-    return finish(w, cross, sketched)
+    y, w, cross = gather(pltpu.with_memory_space_constraint(fields, pltpu.HBM), pltpu.with_memory_space_constraint(probes, pltpu.HBM), n_pts, n_hrs)
+    return finish(w, cross, y)
 
 
 def solution(mesh):

time: 127 us -> 126 us (level)
    pallas_call x1, Pallas kernels: 3.18 us -> 1.5 us  [finish(): pl.pallas_call(output_kernel, out_shape=(jax.ShapeDtypeStruct(y.shape, f3...]
where the time goes in v4:
time: 126 us
  Pallas kernels  125 us (99%)
    pallas_call x1, Pallas kernels, gather(): pl.pallas_call(functools.partial(gather_kernel, n_pts, n_hrs, widths, par...  124 us

profile of v4, /device:TPU:0, one launch (start us, length us, event | category | flops | bytes accessed | tf_op | source)
XLA Modules:
  0.0 125.9 jit_solution(6935727520385491142)
XLA Ops:
  0.6 123.6 %gather.1 = (f32[256,2048]{1,0:T(8,128)S(1)}, f32[256,256]{1,0:T(8,128)S(1)}, f32[256,512]{1,0:T(8,128)S(1)}) custom-call(f32[16,65536]{1,0:T(8,128)} %fields_ref.1, f32[256,512]{1,0:T(8,128)} %probes_hbm.1), custom_call_target="tpu_custom_call" | custom-call | tf_op jit(solution)/shard_map/gather/pallas_call | solution.py:389
  124.3 1.5 %output.1 = (f32[256,2048]{1,0:T(8,128)}, f32[256,512]{1,0:T(8,128)}) custom-call(f32[256,256]{1,0:T(8,128)S(1)} %get-tuple-element.5.w, f32[256,512]{1,0:T(8,128)S(1)} %get-tuple-element.6.cross, f32[256,2048]{1,0:T(8,128)S(1)} %get-tuple-element.7.y), custom_call_target="tpu_custom_call" | custom-call | tf_op jit(solution)/shard_map/output/pallas_call | solution.py:126

commit v5 on v4

--- a/solution.py
+++ b/solution.py
@@ -8,14 +8,13 @@
 from jax.sharding import PartitionSpec as P
 
 HI = lax.Precision.HIGHEST
-YP = lax.Precision.HIGH
 MESH = pl.DeviceIdType.MESH
 VMEM_LIMIT = 24 * 2 ** 20
-POINTS = ((0, 0), (0, 5), (1, 2), (1, 12))
-
-
-def mm(a, b, dims, precision=HI):
-    return lax.dot_general(a, b, (dims, ((), ())), precision=precision, preferred_element_type=jnp.float32)
+POINTS = ((0, 1), (0, 7), (1, 4), (1, 14))
+
+
+def mm(a, b, dims):
+    return lax.dot_general(a, b, (dims, ((), ())), precision=HI, preferred_element_type=jnp.float32)
 
 
 def invert_block(block, between=None):
@@ -77,34 +76,34 @@
     return jnp.concatenate([jnp.where(lane <= srow + 8 * s, outs[s], 0.0) for s in range(n)], axis=0)
 
 
-def packed(k, chips, parts):
-    step = 8 * chips * parts
-    return -(-(k // 2 + k // 4) // step) * step
-
-
-def pack(g, gram, first):
-    k = gram.shape[1]
+def padded(rows, chips):
+    return -(-rows // (8 * chips)) * 8 * chips
+
+
+def pack(g, head, rest, first):
+    k = g.shape[0]
     h, q = k // 2, k // 4
-    for rows, cols, block in (
-        (slice(0, h), slice(0, h), g[:h, :h]),
-        (slice(0, h), slice(h, k), g[h:, h:]),
-        (slice(h, h + q), slice(0, h), g[h:h + q, :h]),
-        (slice(h, h + q), slice(h, k), g[h + q:, :h]),
+    for ref, rows, cols, block in (
+        (head, slice(0, q), slice(0, h), g[:q, :h]),
+        (head, slice(0, q), slice(h, k), g[q:h, :h]),
+        (rest, slice(0, h), slice(0, h), g[h:, h:]),
+        (rest, slice(0, h), slice(h, k), g[h:, :h]),
     ):
-        gram[rows, cols] = block if first else gram[rows, cols] + block
-
-
-def factor(gram, w, between):
+        ref[rows, cols] = block if first else ref[rows, cols] + block
+
+
+def factor(head, rest, w, between):
     k = w.shape[0]
     h, q = k // 2, k // 4
-    top = invert_block(gram[:h, :h], functools.partial(between, 0))
+    first = jnp.concatenate([head[:q, :h], head[:q, h:]], axis=0)
+    top = invert_block(first, functools.partial(between, 0))
     w[:h, :h] = top
     w[:h, h:] = jnp.zeros((h, k - h), jnp.float32)
-    below = jnp.concatenate([gram[h:h + q, :h], gram[h:h + q, h:]], axis=0)
-    side = mm(below, top, ((1,), (1,)))
-    rest = gram[:h, h:] - mm(side, side, ((1,), (1,)))
+    between(0, -1)
+    side = mm(rest[:h, h:], top, ((1,), (1,)))
+    second = rest[:h, :h] - mm(side, side, ((1,), (1,)))
     w[h:, :h] = mm(side, top, ((1,), (0,)))
-    last = invert_block(rest, functools.partial(between, 1))
+    last = invert_block(second, functools.partial(between, 1))
     w[h:, h:] = last
     w[h:, :h] = -mm(last, w[h:, :h], ((1,), (0,)))
 
@@ -267,7 +266,7 @@
     n = n_pts * n_hrs
     m = len(widths)
     panels, scratch = scratch[:m], scratch[m:]
-    flat, probes_ref, part, gram, summed, sk, probes_sem, own_sem, send_sem, recv_sem, *scratch = scratch
+    flat, probes_ref, part, head, rest, head_sum, rest_sum, sk, probes_sem, own_sem, send_sem, recv_sem, *scratch = scratch
     place = Place(n_pts, n_hrs)
     me = place.pts * n_hrs + place.hrs
     rows = fields_ref.shape[0]
@@ -308,10 +307,12 @@
         own.start()
         owns.append(own)
 
-    grams = AllReduce(place, gram, summed, parts, 1.0 / n_points, scratch[:10])
-    crosses = AllReduce(place, part, cross_ref, parts, 1.0 / n_points, scratch[10:])
-    if gram.shape[0] > k // 2 + k // 4:
-        gram[k // 2 + k // 4:, :] = jnp.zeros((gram.shape[0] - k // 2 - k // 4, k), jnp.float32)
+    heads = AllReduce(place, head, head_sum, 1, 1.0 / n_points, scratch[:10])
+    rests = AllReduce(place, rest, rest_sum, 1, 1.0 / n_points, scratch[10:20])
+    crosses = AllReduce(place, part, cross_ref, parts, 1.0 / n_points, scratch[20:])
+    for ref, used in ((head, k // 4), (rest, k // 2)):
+        if ref.shape[0] > used:
+            ref[used:, :] = jnp.zeros((ref.shape[0] - used, k), jnp.float32)
     probes_load.wait()
     for c in range(m):
         owns[c].wait()
@@ -327,9 +328,10 @@
             block = flat[:, :width]
         sketch = mm(probes_ref[...], block, ((1,), (0,)))
         sk[:, cols] = sketch
-        pack(mm(sketch, sketch, ((1,), (1,))), gram, c == 0)
+        pack(mm(sketch, sketch, ((1,), (1,))), head, rest, c == 0)
         if c == m - 1:
-            grams.run(grams.cores)
+            heads.run(heads.cores)
+            rests.run(rests.cores)
         if c < m - 1:
             term = mm(sketch, block, ((1,), (1,)))
             part[...] = term if c == 0 else part[...] + term
@@ -346,26 +348,33 @@
                 part[:, lanes] = term if c == 0 else part[:, lanes] + term
                 if own == 0:
                     crosses.run(crosses.cores)
-    grams.run(grams.chips)
+    heads.run(heads.chips)
+    rests.run(rests.chips)
     crosses.run(crosses.chips)
-    grams.run(grams.layers)
+    heads.run(heads.layers)
+    rests.run(rests.layers)
     crosses.run(crosses.layers)
-    grams.run(grams.spread)
-    grams.run(grams.share)
-    grams.finish()
-    todo = {POINTS[p]: functools.partial(step, p % parts) for p, step in enumerate([crosses.spread] * parts + [crosses.share] * parts)}
-
+    heads.run(heads.spread)
+    rests.run(rests.spread)
+    heads.run(heads.share)
+    heads.finish()
+    todo = {(0, 3): [functools.partial(rests.share, 0)], (0, -1): [rests.finish]}
+    steps = [functools.partial(crosses.spread, p) for p in range(parts)] + [functools.partial(crosses.share, p) for p in range(parts)]
+    for point, step in zip(POINTS, steps):
+        todo.setdefault(point, []).append(step)
 
     def between(block, panel):
         if (block, panel) in todo:
-            todo[block, panel]()
-
-    factor(summed, w_ref, between)
+            for step in todo[block, panel]:
+                step()
+
+    factor(head_sum, rest_sum, w_ref, between)
     step = 512
     for t in range(0, local, step):
-        y_ref[:, t:t + step] = mm(w_ref[...], sk[:, t:t + step], ((1,), (0,)), YP)
+        y_ref[:, t:t + step] = mm(w_ref[...], sk[:, t:t + step], ((1,), (0,)))
     crosses.finish()
-    grams.drain()
+    heads.drain()
+    rests.drain()
     crosses.drain()
     for c in range(m):
         most = panels[c].at[pl.ds(0, n - 1)]
@@ -381,7 +390,7 @@
     m = len(widths)
     cores, low, chips, layers = split(n_pts, n_hrs)
     parts = 2 if k % (2 * chips * 8) == 0 else 1
-    gram_rows = packed(k, chips, parts)
+    sizes = (padded(k // 4, chips), padded(k // 2, chips))
     v = pl.BlockSpec(memory_space=pltpu.VMEM)
     far = pl.BlockSpec(memory_space=pltpu.HBM)
     dma = pltpu.SemaphoreType.DMA
@@ -398,11 +407,10 @@
             pltpu.VMEM((hours, max(widths)) if rows % 8 else (8, 128), f32),
             pltpu.VMEM((k, hours), f32),
             pltpu.VMEM((k, hours), f32),
-            pltpu.VMEM((gram_rows, k), f32),
-            pltpu.VMEM((gram_rows, k), f32),
+            *(pltpu.VMEM((size, k), f32) for size in sizes * 2),
             pltpu.VMEM((k, local), f32),
             dma(()), dma((m,)), dma((m,)), dma((m,)),
-            *reduce_shapes(n_pts, n_hrs, gram_rows, k, parts),
+            *(shape for size in sizes for shape in reduce_shapes(n_pts, n_hrs, size, k, 1)),
             *reduce_shapes(n_pts, n_hrs, k, hours, parts),
         ],
         compiler_params=pltpu.CompilerParams(collective_id=1, has_side_effects=True, vmem_limit_bytes=VMEM_LIMIT),
@@ -413,7 +421,7 @@
 def pieces(local):
     if local % 128 or local < 1024:
         return (local,)
-    last = 128
+    last = 256
     big = 512
     rest = local - last
     widths = []

time: 126 us -> 125 us (level)
    pallas_call x1, Pallas kernels: 124 us -> 122 us  [gather(): pl.pallas_call(functools.partial(gather_kernel, n_pts, n_hrs, widths, par...]
where the time goes in v5:
time: 125 us
  Pallas kernels  124 us (99%)
    pallas_call x1, Pallas kernels, gather(): pl.pallas_call(functools.partial(gather_kernel, n_pts, n_hrs, widths, par...  122 us

profile of v5, /device:TPU:0, one launch (start us, length us, event | category | flops | bytes accessed | tf_op | source)
XLA Modules:
  0.0 124.5 jit_solution(4856307644643873435)
XLA Ops:
  0.6 122.2 %gather.1 = (f32[256,2048]{1,0:T(8,128)S(1)}, f32[256,256]{1,0:T(8,128)S(1)}, f32[256,512]{1,0:T(8,128)S(1)}) custom-call(f32[16,65536]{1,0:T(8,128)} %fields_ref.1, f32[256,512]{1,0:T(8,128)} %probes_hbm.1), custom_call_target="tpu_custom_call" | custom-call | tf_op jit(solution)/shard_map/gather/pallas_call | solution.py:398
  122.9 1.5 %output.1 = (f32[256,2048]{1,0:T(8,128)}, f32[256,512]{1,0:T(8,128)}) custom-call(f32[256,256]{1,0:T(8,128)S(1)} %get-tuple-element.5.w, f32[256,512]{1,0:T(8,128)S(1)} %get-tuple-element.6.cross, f32[256,2048]{1,0:T(8,128)S(1)} %get-tuple-element.7.y), custom_call_target="tpu_custom_call" | custom-call | tf_op jit(solution)/shard_map/output/pallas_call | solution.py:125

commit v6 on v5

--- a/solution.py
+++ b/solution.py
@@ -134,10 +134,10 @@
 
 
 class Place:
-    def __init__(self, n_pts, n_hrs):
+    def __init__(self, n_pts, n_hrs, pair):
         self.pts, self.hrs = lax.axis_index("pts"), lax.axis_index("hrs")
         self.n_pts, self.n_hrs = n_pts, n_hrs
-        self.cores, self.low, self.chips, self.layers = split(n_pts, n_hrs)
+        self.cores, self.low, self.chips, self.layers = split(n_pts, n_hrs, pair)
         self.core = lax.rem(self.hrs, self.cores)
         self.layer = self.pts // self.low
         self.chip = (self.hrs // self.cores) * self.low + lax.rem(self.pts, self.low)
@@ -146,16 +146,16 @@
         return (layer * self.low + lax.rem(chip, self.low), (chip // self.low) * self.cores + core)
 
 
-def split(n_pts, n_hrs):
-    cores = 2 if n_hrs % 2 == 0 else 1
+def split(n_pts, n_hrs, pair):
+    cores = 2 if pair and n_hrs % 2 == 0 else 1
     low = 1
     while n_pts % (low * 2) == 0 and low * 2 * low * 2 <= n_pts:
         low *= 2
     return cores, low, (n_hrs // cores) * low, n_pts // low
 
 
-def reduce_shapes(n_pts, n_hrs, rows, width, parts):
-    cores, low, chips, layers = split(n_pts, n_hrs)
+def reduce_shapes(n_pts, n_hrs, pair, rows, width, parts):
+    cores, low, chips, layers = split(n_pts, n_hrs, pair)
     lanes = width // cores
     h = rows // parts
     q = h // chips
@@ -267,7 +267,7 @@
     m = len(widths)
     panels, scratch = scratch[:m], scratch[m:]
     flat, probes_ref, part, head, rest, head_sum, rest_sum, sk, probes_sem, own_sem, send_sem, recv_sem, *scratch = scratch
-    place = Place(n_pts, n_hrs)
+    place = Place(n_pts, n_hrs, True)
     me = place.pts * n_hrs + place.hrs
     rows = fields_ref.shape[0]
     local = sum(widths)
@@ -307,7 +307,7 @@
         own.start()
         owns.append(own)
 
-    heads = AllReduce(place, head, head_sum, 1, 1.0 / n_points, scratch[:10])
+    heads = AllReduce(Place(n_pts, n_hrs, False), head, head_sum, 1, 1.0 / n_points, scratch[:10])
     rests = AllReduce(place, rest, rest_sum, 1, 1.0 / n_points, scratch[10:20])
     crosses = AllReduce(place, part, cross_ref, parts, 1.0 / n_points, scratch[20:])
     for ref, used in ((head, k // 4), (rest, k // 2)):
@@ -330,7 +330,7 @@
         sk[:, cols] = sketch
         pack(mm(sketch, sketch, ((1,), (1,))), head, rest, c == 0)
         if c == m - 1:
-            heads.run(heads.cores)
+            heads.run(heads.chips)
             rests.run(rests.cores)
         if c < m - 1:
             term = mm(sketch, block, ((1,), (1,)))
@@ -348,13 +348,14 @@
                 part[:, lanes] = term if c == 0 else part[:, lanes] + term
                 if own == 0:
                     crosses.run(crosses.cores)
-    heads.run(heads.chips)
     rests.run(rests.chips)
     crosses.run(crosses.chips)
     heads.run(heads.layers)
     rests.run(rests.layers)
-    crosses.run(crosses.layers)
+    crosses.layers(0)
     heads.run(heads.spread)
+    for p in range(1, parts):
+        crosses.layers(p)
     rests.run(rests.spread)
     heads.run(heads.share)
     heads.finish()
@@ -388,9 +389,9 @@
     local = n_points // n
     widths = pieces(local)
     m = len(widths)
-    cores, low, chips, layers = split(n_pts, n_hrs)
+    _, _, chips, _ = split(n_pts, n_hrs, True)
     parts = 2 if k % (2 * chips * 8) == 0 else 1
-    sizes = (padded(k // 4, chips), padded(k // 2, chips))
+    sizes = (padded(k // 4, split(n_pts, n_hrs, False)[2]), padded(k // 2, chips))
     v = pl.BlockSpec(memory_space=pltpu.VMEM)
     far = pl.BlockSpec(memory_space=pltpu.HBM)
     dma = pltpu.SemaphoreType.DMA
@@ -410,8 +411,9 @@
             *(pltpu.VMEM((size, k), f32) for size in sizes * 2),
             pltpu.VMEM((k, local), f32),
             dma(()), dma((m,)), dma((m,)), dma((m,)),
-            *(shape for size in sizes for shape in reduce_shapes(n_pts, n_hrs, size, k, 1)),
-            *reduce_shapes(n_pts, n_hrs, k, hours, parts),
+            *reduce_shapes(n_pts, n_hrs, False, sizes[0], k, 1),
+            *reduce_shapes(n_pts, n_hrs, True, sizes[1], k, 1),
+            *reduce_shapes(n_pts, n_hrs, True, k, hours, parts),
         ],
         compiler_params=pltpu.CompilerParams(collective_id=1, has_side_effects=True, vmem_limit_bytes=VMEM_LIMIT),
         name="gather",

time: 125 us -> 124 us (level)
  no operation moved by 1% of the time
where the time goes in v6:
time: 124 us
  Pallas kernels  123 us (99%)
    pallas_call x1, Pallas kernels, gather(): pl.pallas_call(functools.partial(gather_kernel, n_pts, n_hrs, widths, par...  121 us

profile of v6, /device:TPU:0, one launch (start us, length us, event | category | flops | bytes accessed | tf_op | source)
XLA Modules:
  0.0 123.6 jit_solution(9324760347288630118)
XLA Ops:
  0.6 121.3 %gather.1 = (f32[256,2048]{1,0:T(8,128)S(1)}, f32[256,256]{1,0:T(8,128)S(1)}, f32[256,512]{1,0:T(8,128)S(1)}) custom-call(f32[16,65536]{1,0:T(8,128)} %fields_ref.1, f32[256,512]{1,0:T(8,128)} %probes_hbm.1), custom_call_target="tpu_custom_call" | custom-call | tf_op jit(solution)/shard_map/gather/pallas_call | solution.py:399
  121.9 1.5 %output.1 = (f32[256,2048]{1,0:T(8,128)}, f32[256,512]{1,0:T(8,128)}) custom-call(f32[256,256]{1,0:T(8,128)S(1)} %get-tuple-element.5.w, f32[256,512]{1,0:T(8,128)S(1)} %get-tuple-element.6.cross, f32[256,2048]{1,0:T(8,128)S(1)} %get-tuple-element.7.y), custom_call_target="tpu_custom_call" | custom-call | tf_op jit(solution)/shard_map/output/pallas_call | solution.py:125

commit v7 on v6

--- a/solution.py
+++ b/solution.py
@@ -80,16 +80,23 @@
     return -(-rows // (8 * chips)) * 8 * chips
 
 
-def pack(g, head, rest, first):
-    k = g.shape[0]
+def add_to(ref, blocks, first):
+    for rows, cols, block in blocks:
+        ref[rows, cols] = block if first else ref[rows, cols] + block
+
+
+def add_head(sketch, head, first):
+    k = sketch.shape[0]
     h, q = k // 2, k // 4
-    for ref, rows, cols, block in (
-        (head, slice(0, q), slice(0, h), g[:q, :h]),
-        (head, slice(0, q), slice(h, k), g[q:h, :h]),
-        (rest, slice(0, h), slice(0, h), g[h:, h:]),
-        (rest, slice(0, h), slice(h, k), g[h:, :h]),
-    ):
-        ref[rows, cols] = block if first else ref[rows, cols] + block
+    g = mm(sketch[:h], sketch[:h], ((1,), (1,)))
+    add_to(head, ((slice(0, q), slice(0, h), g[:q]), (slice(0, q), slice(h, k), g[q:])), first)
+
+
+def add_rest(sketch, rest, first):
+    k = sketch.shape[0]
+    h = k // 2
+    g = mm(sketch[h:], sketch, ((1,), (1,)))
+    add_to(rest, ((slice(0, h), slice(0, h), g[:, h:]), (slice(0, h), slice(h, k), g[:, :h])), first)
 
 
 def factor(head, rest, w, between):
@@ -328,9 +335,11 @@
             block = flat[:, :width]
         sketch = mm(probes_ref[...], block, ((1,), (0,)))
         sk[:, cols] = sketch
-        pack(mm(sketch, sketch, ((1,), (1,))), head, rest, c == 0)
+        add_head(sketch, head, c == 0)
         if c == m - 1:
             heads.run(heads.chips)
+        add_rest(sketch, rest, c == 0)
+        if c == m - 1:
             rests.run(rests.cores)
         if c < m - 1:
             term = mm(sketch, block, ((1,), (1,)))

time: 124 us -> 124 us (level)
  no operation moved by 1% of the time
where the time goes in v7:
time: 124 us
  Pallas kernels  123 us (99%)
    pallas_call x1, Pallas kernels, gather(): pl.pallas_call(functools.partial(gather_kernel, n_pts, n_hrs, widths, par...  121 us

profile of v7, /device:TPU:0, one launch (start us, length us, event | category | flops | bytes accessed | tf_op | source)
XLA Modules:
  0.0 123.5 jit_solution(10336250980940459756)
XLA Ops:
  0.6 121.2 %gather.1 = (f32[256,2048]{1,0:T(8,128)S(1)}, f32[256,256]{1,0:T(8,128)S(1)}, f32[256,512]{1,0:T(8,128)S(1)}) custom-call(f32[16,65536]{1,0:T(8,128)} %fields_ref.1, f32[256,512]{1,0:T(8,128)} %probes_hbm.1), custom_call_target="tpu_custom_call" | custom-call | tf_op jit(solution)/shard_map/gather/pallas_call | solution.py:408
  121.9 1.5 %output.1 = (f32[256,2048]{1,0:T(8,128)}, f32[256,512]{1,0:T(8,128)}) custom-call(f32[256,256]{1,0:T(8,128)S(1)} %get-tuple-element.5.w, f32[256,512]{1,0:T(8,128)S(1)} %get-tuple-element.6.cross, f32[256,2048]{1,0:T(8,128)S(1)} %get-tuple-element.7.y), custom_call_target="tpu_custom_call" | custom-call | tf_op jit(solution)/shard_map/output/pallas_call | solution.py:132
